TPU v7x, 32 devices: a whole 2x2x4 slice. The times are simulated.
32 devices in a mesh: seq: 8 (over z, x), head: 4 (over y, core).
Axes of the slice: x: 2, y: 2, z: 4, core: 2. Of those that a mesh axis runs over, the one named last changes fastest.
Arguments:
- query: bfloat16 [4096, 4096], P(('seq', 'head')), may hold values from -6 to 6
- key: bfloat16 [4096, 1024], P(('seq', 'head')), may hold values from -6 to 6
- value: bfloat16 [4096, 1024], P(('seq', 'head')), may hold values from -6 to 6
- out: bfloat16 [4096, 4096], P(('seq', 'head')), may hold values from -4 to 4
- output_gradient: bfloat16 [4096, 4096], P(('seq', 'head')), may hold values from -6 to 6
- log_sum_exp: float32 [4096, 32], P(('seq', 'head')), may hold values from 4 to 7
- segment_ids: int32 [4096], replicated, may hold values from 0 to 3, never falling along the last dimension, each value on 1 to 1536 neighbouring positions
Outputs:
- d_query: bfloat16 [4096, 4096], P(('seq', 'head'))
- key_gradient: bfloat16 [4096, 1024], P(('seq', 'head'))
- value_gradient: bfloat16 [4096, 1024], P(('seq', 'head'))
Inputs may be any that keep to these rules, and one draw needn't show every extreme that they name: `segment_ids`: never falls along the positions; a document holds at most 1536 positions, and one holds exactly 1536.
All inputs are finite; a program needn't handle non-finite values.
Results may differ from a plain program's by a relative error of at most 0.0071.
Values may be sent and summed in bfloat16 or wider, within the bound.
A program may use at most 128 MiB of HBM per device.

v0:
```python
import functools
import math

import jax
import jax.numpy as jnp
from jax import lax
from jax.experimental import pallas as pl
from jax.experimental.pallas import tpu as pltpu
from jax.sharding import PartitionSpec as P

HEAD_SIZE = 128
REACH = 3
TILE = 256
LOG2E = math.log2(math.e)
MESH = pl.DeviceIdType.MESH
NT = (((1,), (1,)), ((), ()))


def dot(a, b):
    return jnp.dot(a, b, preferred_element_type=jnp.float32)


def dot_nt(a, b):
    return lax.dot_general(a, b, NT, preferred_element_type=jnp.float32)


def kernel(
    n, seqs, groups, width,
    q_ref, e_ref, k_ref, v_ref, st_ref, start_ref,
    dq_out, dk_out, dv_out,
    qb, eb, stb, kv, dqt, acck, accv, ownk, ownv, part_s, part_r, dqs, dks, dvs,
    loc_sem, in_s, in_r, fw_s, fw_r, pt_s, pt_r, out_s, out_r,
):
    s = lax.axis_index("seq")
    h = lax.axis_index("head")
    rows = q_ref.shape[0]
    block = rows * n
    cols = q_ref.shape[1] // n
    kcols = k_ref.shape[1] // n
    hd = HEAD_SIZE
    gw = width * hd
    halves = block // TILE
    scale = 1.0 / math.sqrt(hd)
    heads = groups * width

    def at(index, size):
        return pl.ds(index * size if isinstance(index, int) else pl.multiple_of(index * size, size), size)

    side = s + 1 - 2 * lax.rem(s, 2)
    even = lax.rem(s, 2) == 0
    odd = lax.rem(s, 2) == 1
    has_up, has_down = s + 2 < seqs, s >= 2

    barrier = pltpu.get_barrier_semaphore()
    for r in range(1, n):
        pl.semaphore_signal(barrier, inc=1, device_id={"head": lax.rem(h + r, n)}, device_id_type=MESH)
    pl.semaphore_signal(barrier, inc=1, device_id={"seq": side}, device_id_type=MESH)

    @pl.when(has_up)
    def _():
        pl.semaphore_signal(barrier, inc=1, device_id={"seq": s + 2}, device_id_type=MESH)

    @pl.when(has_down)
    def _():
        pl.semaphore_signal(barrier, inc=1, device_id={"seq": s - 2}, device_id_type=MESH)

    pl.semaphore_wait(barrier, n + jnp.minimum(s // 2, 1) + jnp.minimum((seqs - 1 - s) // 2, 1))

    def entry(kind, owner, me):
        if kind == 0:
            return st_ref.at[owner], stb.at[:, at(me, rows)]
        if kind < first_wide:
            g, which = (kind - 1) // 2, (kind - 1) % 2
            from_cols = pl.ds(pl.multiple_of(owner * kcols + g * hd, hd), hd)
            return (k_ref, v_ref)[which].at[:, from_cols], kv.at[0, g, which, at(me, rows), :]
        g, which = (kind - first_wide) // 2, (kind - first_wide) % 2
        src, dst = ((q_ref, qb), (e_ref, eb))[which]
        from_cols = pl.ds(pl.multiple_of(owner * cols + g * gw, hd), gw)
        return src.at[:, from_cols], dst.at[at(me, rows), pl.ds(g * gw, gw)]

    first_wide = 1 + 2 * groups
    kinds = 1 + 4 * groups

    def entry_copy(kind, r):
        peer = lax.rem(h + r, n)
        src, dst = entry(kind, peer, h)
        return pltpu.make_async_remote_copy(
            src_ref=src, dst_ref=dst, send_sem=in_s.at[kind, r - 1], recv_sem=in_r.at[kind, r - 1],
            device_id={"head": peer}, device_id_type=MESH)

    def entry_own(kind):
        src, dst = entry(kind, h, h)
        return pltpu.make_async_copy(src, dst, loc_sem.at[kind])

    for kind in tuple(range(1, first_wide)) + (0,) + tuple(range(first_wide, kinds)):
        entry_own(kind).start()
        for r in range(1, n):
            entry_copy(kind, r).start()

    def entry_wait(kind):
        entry_own(kind).wait()
        for r in range(1, n):
            entry_copy(kind, r).wait_recv()

    def hand(g, step, slot, to_slot, to):
        return pltpu.make_async_remote_copy(
            src_ref=kv.at[slot, g], dst_ref=kv.at[to_slot, g], send_sem=fw_s.at[g, step],
            recv_sem=fw_r.at[g, to_slot - 1], device_id={"seq": to}, device_id_type=MESH)

    def hand_steps(g):
        return (
            (has_up, hand(g, 0, 0, 2, s + 2)),
            (even, hand(g, 1, 0, 1, side)),
            (has_down & odd, hand(g, 2, 2, 1, side)),
            (has_down & even, hand(g, 2, 2, 3, side)),
            (has_down & even & has_up, hand(g, 3, 1, 3, s + 2)),
        )

    def hand_start(g, steps):
        for i in steps:
            cond, copy = hand_steps(g)[i]

            @pl.when(cond)
            def _():
                copy.start()

    def got(g, d):
        @pl.when(s >= d)
        def _():
            hand(g, 0, 0, d, side).wait_recv()

    def back(g, d, into, to):
        return pltpu.make_async_remote_copy(
            src_ref=part_s.at[g, d - 1], dst_ref=part_r.at[g, into], send_sem=pt_s.at[g, d - 1],
            recv_sem=pt_r.at[g, into], device_id={"seq": to}, device_id_type=MESH)

    def join(g, into):
        back(g, 1, into, side).wait_recv()
        acck[...] += part_r[g, into, 0].astype(jnp.float32)
        accv[...] += part_r[g, into, 1].astype(jnp.float32)

    def put(g, d):
        part_s[g, d - 1, 0] = acck[...].astype(jnp.bfloat16)
        part_s[g, d - 1, 1] = accv[...].astype(jnp.bfloat16)

    def pass_back(g, d):
        if d == 3:
            put(g, 3)

            @pl.when(even)
            def _():
                back(g, 3, 0, s - 2).start()

            @pl.when(odd)
            def _():
                back(g, 3, 1, side).start()
        elif d == 1:
            @pl.when(has_down & even & has_up)
            def _():
                join(g, 0)

            put(g, 1)

            @pl.when(even)
            def _():
                back(g, 1, 1, side).start()

            @pl.when(odd)
            def _():
                back(g, 1, 3, side).start()
        else:
            join(g, 1)
            put(g, 2)
            back(g, 2, 2, s - 2).start()

    def leave(which, g, owner):
        src, dst, size, full = ((dqs, dq_out, gw, cols), (dks, dk_out, hd, kcols), (dvs, dv_out, hd, kcols))[which]
        to_cols = pl.ds(pl.multiple_of(h * full + g * size, hd), size)
        return src.at[at(owner, rows), pl.ds(g * size, size)], dst.at[:, to_cols]

    def leave_copy(which, g, r):
        peer = lax.rem(h + r, n)
        src, dst = leave(which, g, peer)
        return pltpu.make_async_remote_copy(
            src_ref=src, dst_ref=dst, send_sem=out_s.at[which, g, r - 1], recv_sem=out_r.at[which, g, r - 1],
            device_id={"head": peer}, device_id_type=MESH)

    def leave_own(which, g):
        src, dst = leave(which, g, h)
        return pltpu.make_async_copy(src, dst, loc_sem.at[kinds + which * groups + g])

    def leave_start(which, g):
        for r in range(1, n):
            leave_copy(which, g, r).start()
        leave_own(which, g).start()

    for g in range(groups):
        entry_wait(1 + 2 * g)
        entry_wait(2 + 2 * g)
        hand_start(g, (0, 1))
    entry_wait(0)

    def relay_two(g):
        got(g, 2)
        hand_start(g, (2, 3))

    def relay_one(g):
        got(g, 1)
        hand_start(g, (4,))

    row_at = lax.broadcasted_iota(jnp.int32, (TILE, TILE), 0)
    col_at = lax.broadcasted_iota(jnp.int32, (TILE, TILE), 1)

    def tile(g, d, hf, qt):
        k_rows, q_rows = at(hf, TILE), at(qt, TILE)
        key, val = kv[d, g, 0, k_rows, :], kv[d, g, 1, k_rows, :]
        key_t = key.T
        first = start_ref[0:1, q_rows] - (hf * TILE - d * block)
        allowed = row_at >= first
        if d == 0:
            allowed &= row_at + (hf - qt) * TILE <= col_at
        add_k = add_v = None
        for m in range(width):
            hcol = pl.ds((g * width + m) * hd, hd)
            query, grad = qb[q_rows, hcol], eb[q_rows, hcol]
            lse = stb[g * width + m : g * width + m + 1, q_rows]
            delta = stb[heads + g * width + m : heads + g * width + m + 1, q_rows]
            scores = dot_nt(key, query)
            probs = jnp.exp2(jnp.where(allowed, scores * (scale * LOG2E) - lse, -jnp.inf))
            dprobs = dot_nt(val, grad)
            dscores = (probs * (dprobs - delta)).astype(jnp.bfloat16)
            one_v = dot(probs.astype(jnp.bfloat16), grad)
            one_k = dot(dscores, query)
            add_v = one_v if m == 0 else add_v + one_v
            add_k = one_k if m == 0 else add_k + one_k
            dqt[m, :, q_rows] += dot(key_t, dscores)
        acck[k_rows, :] += add_k
        accv[k_rows, :] += add_v

    def compute(g, d):
        acck[...] = jnp.zeros_like(acck)
        accv[...] = jnp.zeros_like(accv)

        for hf in range(halves):
            low = hf if d == 0 else 0
            high = hf + 1 if d == REACH else halves
            for qt in range(low, high):
                tile(g, d, hf, qt)

    def finish(g):
        for cond, into in ((even, 3), (has_up, 2)):
            @pl.when(cond)
            def _():
                back(g, 1, into, side).wait_recv()
                ownk[g] += part_r[g, into, 0].astype(jnp.float32)
                ownv[g] += part_r[g, into, 1].astype(jnp.float32)

        dks[:, g * hd : (g + 1) * hd] = (ownk[g] * scale).astype(jnp.bfloat16)
        dvs[:, g * hd : (g + 1) * hd] = ownv[g].astype(jnp.bfloat16)
        leave_start(1, g)
        leave_start(2, g)

    relay_two(0)
    for g in range(groups):
        if g == 0:
            relay_two(1)
            relay_one(0)
        entry_wait(first_wide + 2 * g)
        entry_wait(first_wide + 1 + 2 * g)
        dqt[...] = jnp.zeros_like(dqt)
        for step, d in enumerate((0, 3, 1, 2) if g == 0 else (3, 1, 2, 0)):
            if d == 0:
                compute(g, 0)
                ownk[g] = acck[...]
                ownv[g] = accv[...]
                if g == 0:
                    relay_one(1)
            else:
                if d == 3:
                    got(g, 3)

                @pl.when(s >= d)
                def _():
                    compute(g, d)
                    pass_back(g, d)
            if g > 0 and step == 1:
                finish(g - 1)
        for m in range(width):
            here = (g * width + m) * hd
            dqs[:, here : here + hd] = (dqt[m] * scale).T.astype(jnp.bfloat16)
        leave_start(0, g)
    finish(groups - 1)

    for which in range(3):
        for g in range(groups):
            leave_own(which, g).wait()
            for r in range(1, n):
                leave_copy(which, g, r).wait()
    for kind in range(kinds):
        for r in range(1, n):
            entry_copy(kind, r).wait_send()
    for g in range(groups):
        for cond, copy in hand_steps(g):
            @pl.when(cond)
            def _():
                copy.wait_send()

        for d in range(1, REACH + 1):
            @pl.when(s >= d)
            def _():
                back(g, d, 0, side).wait_send()


def shards(query, key, value, out, output_gradient, log_sum_exp, segment_ids):
    n, seqs = lax.axis_size("head"), lax.axis_size("seq")
    hd = HEAD_SIZE
    rows = query.shape[0]
    block = rows * n
    cols, kcols = query.shape[1] // n, key.shape[1] // n
    groups, width = kcols // hd, cols // kcols
    heads = groups * width
    delta = jnp.sum(
        (output_gradient.astype(jnp.float32) * out.astype(jnp.float32)).reshape(rows, -1, hd), axis=2
    )
    stats = jnp.concatenate(
        [(log_sum_exp * LOG2E).T.reshape(n, heads, rows), delta.T.reshape(n, heads, rows)], axis=1
    )
    base = lax.axis_index("seq") * block
    mine = lax.dynamic_slice_in_dim(segment_ids, base, block, 0)
    start = jnp.sum((segment_ids[:, None] < mine[None, :]).astype(jnp.int32), axis=0)[None, :] - base
    bf16, f32 = jnp.bfloat16, jnp.float32
    kinds = 1 + 4 * groups
    vmem = pl.BlockSpec(memory_space=pltpu.VMEM)
    dma = pltpu.SemaphoreType.DMA
    return pl.pallas_call(
        functools.partial(kernel, n, seqs, groups, width),
        out_shape=[
            jax.ShapeDtypeStruct(query.shape, bf16),
            jax.ShapeDtypeStruct(key.shape, bf16),
            jax.ShapeDtypeStruct(value.shape, bf16),
        ],
        in_specs=[vmem] * 6,
        out_specs=[vmem] * 3,
        scratch_shapes=[
            pltpu.VMEM((block, cols), bf16),
            pltpu.VMEM((block, cols), bf16),
            pltpu.VMEM((2 * heads, block), f32),
            pltpu.VMEM((REACH + 1, groups, 2, block, hd), bf16),
            pltpu.VMEM((width, hd, block), f32),
            pltpu.VMEM((block, hd), f32),
            pltpu.VMEM((block, hd), f32),
            pltpu.VMEM((groups, block, hd), f32),
            pltpu.VMEM((groups, block, hd), f32),
            pltpu.VMEM((groups, REACH, 2, block, hd), bf16),
            pltpu.VMEM((groups, REACH + 1, 2, block, hd), bf16),
            pltpu.VMEM((block, cols), bf16),
            pltpu.VMEM((block, kcols), bf16),
            pltpu.VMEM((block, kcols), bf16),
            dma((kinds + 3 * groups,)),
            dma((kinds, n - 1)),
            dma((kinds, n - 1)),
            dma((groups, REACH + 1)),
            dma((groups, REACH)),
            dma((groups, REACH)),
            dma((groups, REACH + 1)),
            dma((3, groups, n - 1)),
            dma((3, groups, n - 1)),
        ],
        compiler_params=pltpu.CompilerParams(collective_id=0, has_side_effects=True),
    )(query, output_gradient, key, value, stats, start)


def solution(mesh):
    placed = (P(("seq", "head"), None),) * 6 + (P(),)
    return jax.shard_map(
        lambda *a: tuple(shards(*a)),
        mesh=mesh,
        in_specs=placed,
        out_specs=(P(("seq", "head"), None),) * 3,
        check_vma=False,
    )
```

profile of v0, /device:TPU:13, one launch (start us, length us, event | category | flops | bytes accessed | tf_op | source)
XLA Modules:
  0.0 84.9 jit_solution(1954015998736570382)
XLA Ops:
  0.6 1.8 %multiply_bitcast_fusion = f32[16,8,32,128]{3,1,2,0:T(8,128)S(1)} fusion(bf16[128,4096]{1,0:T(8,128)(2,1)} %param.10, bf16[128,4096]{1,0:T(8,128)(2,1)} %e_ref.1), kind=kLoop, calls=%fused_computation.1 | loop fusion | flops 1572864 | bytes 4194304
  2.4 0.4 copy.12
  2.8 0.0 copy-start.2
  2.8 0.0 copy-start.3
  2.8 0.6 reduce_sum.18
  3.4 0.1 copy.11
  3.5 0.0 copy-done.2
  3.5 0.6 pad_maximum_fusion.st_ref
  4.2 0.0 copy-done.3
  4.2 0.1 dynamic_slice.3
  4.2 1.0 %convert_reduce_fusion = s32[512]{0:T(512)S(1)} fusion(s32[512]{0:T(512)S(1)} %dynamic_slice.3, s32[4096]{0:T(1024)S(1)} %copy-done.3), kind=kLoop, calls=%fused_computation | loop fusion | flops 6290944 | bytes 20480 | tf_op jit(solution)/shard_map/reduce_sum | solution.py:330
  5.2 0.6 broadcast_subtract_fusion
  5.8 75.4 %shard_map.94 = (bf16[128,4096]{1,0:T(8,128)(2,1)}, bf16[128,1024]{1,0:T(8,128)(2,1)}, bf16[128,1024]{1,0:T(8,128)(2,1)}) custom-call(bf16[128,4096]{1,0:T(8,128)(2,1)} %q_ref.1, bf16[128,4096]{1,0:T(8,128)(2,1)} %e_ref.1, bf16[128,1024]{1,0:T(8,128)(2,1)} %k_ref.1, bf16[128,1024]{1,0:T(8,128)(2,1)} %v_ref.1, f32[4,16,128]{2,1,0:T(8,128)} %pad_maximum_fusion.st_ref, ...), custom_call_target="tpu_custom_call" | custom-call | tf_op jit(solution)/shard_map/pallas_call | solution.py:335
  81.2 0.0 copy-start.1
  81.2 0.0 copy-start
  81.2 2.3 %copy.16 = bf16[128,4096]{1,0:T(8,128)(2,1)} copy(bf16[128,4096]{1,0:T(8,128)(2,1)} %get-tuple-element.6) | data formatting | bytes 2097152
  83.5 0.0 copy-done.1
  83.5 0.7 copy.17
  84.2 0.0 copy-done
  84.2 0.7 copy.18
  (1 shorter events, 0.0 us)
Async XLA Ops:
  2.8 0.7 copy-start.2
  2.8 1.3 %copy-start.3 = (s32[4096]{0:T(1024)S(1)}, s32[4096]{0:T(1024)}, u32[]{:S(2)}) copy-start(s32[4096]{0:T(1024)} %param.13) | copy-start | bytes 49156
  81.2 2.4 %copy-start.1 = (bf16[128,1024]{1,0:T(8,128)(2,1)S(1)}, bf16[128,1024]{1,0:T(8,128)(2,1)}, u32[]{:S(2)}) copy-start(bf16[128,1024]{1,0:T(8,128)(2,1)} %get-tuple-element.7) | copy-start | bytes 786436
  81.2 3.1 %copy-start = (bf16[128,1024]{1,0:T(8,128)(2,1)S(1)}, bf16[128,1024]{1,0:T(8,128)(2,1)}, u32[]{:S(2)}) copy-start(bf16[128,1024]{1,0:T(8,128)(2,1)} %get-tuple-element.8) | copy-start | bytes 786436
where the time goes:
time: 85.2 us; the launch traced here: 84.9 us
  Pallas kernels  75.4 us (88%)
  other arithmetic  4.59 us (5%)
  local copies, waits for them, and re-layouts  4.29 us (5%)
    pallas_call x1, Pallas kernels, shards(): pl.pallas_call(functools.partial(kernel, n, seqs, groups, width), out_sha...  75.4 us
    unnamed x12, local copies, waits for them, and re-layouts  4.16 us
    unnamed x1, other arithmetic  1.8 us

commit v1 on v0

v1 whole, which is shorter than its diff:
```python
import functools
import math

import jax
import jax.numpy as jnp
from jax import lax
from jax.experimental import pallas as pl
from jax.experimental.pallas import tpu as pltpu
from jax.sharding import PartitionSpec as P

HEAD_SIZE = 128
BACK = 6
LOG2E = math.log2(math.e)
MESH = pl.DeviceIdType.MESH
NT = (((1,), (1,)), ((), ()))


def dot(a, b):
    return jnp.dot(a, b, preferred_element_type=jnp.float32)


def dot_nt(a, b):
    return lax.dot_general(a, b, NT, preferred_element_type=jnp.float32)


def kernel(
    n, seqs, width,
    q_ref, e_ref, o_ref, k_ref, v_ref, lse_ref, seg_ref,
    dq_out, dk_out, dv_out,
    qb, eb, stl, stb, kvb, segk, segq, dqt, acck, accv, ps, pr, dqs, dks, dvs,
    loc_sem, in_s, in_r, fw_s, fw_r, pt_s, pt_r, out_s, out_r,
):
    s = lax.axis_index("seq")
    h = lax.axis_index("head")
    rows = q_ref.shape[0]
    hd = HEAD_SIZE
    tile = 2 * rows
    size = 2 * n
    tiles = size // 2
    window = tiles + BACK
    cols = width * hd
    pairs = width // 2
    pcols = cols // pairs
    scale = 1.0 / math.sqrt(hd)
    f32, bf16 = jnp.float32, jnp.bfloat16

    def at(index, length):
        return pl.ds(index * length if isinstance(index, int) else pl.multiple_of(index * length, length), length)

    plane = s // 2
    p = lax.rem(s, 2) * n + h
    own = p // 2
    has_up, has_down, has_two = s + 2 < seqs, s >= 2, s >= 4

    def dev(index):
        return {"seq": s - lax.rem(s, 2) + index // n, "head": lax.rem(index, n)}

    def flip(value, by):
        bit = 1
        while bit <= by:
            if (by // bit) % 2:
                value = value + bit - 2 * bit * lax.rem(value // bit, 2)
            bit *= 2
        return value

    barrier = pltpu.get_barrier_semaphore()
    for by in range(1, size):
        pl.semaphore_signal(barrier, inc=1, device_id=dev(flip(p, by)), device_id_type=MESH)

    @pl.when(has_up)
    def _():
        pl.semaphore_signal(barrier, inc=1, device_id={"seq": s + 2}, device_id_type=MESH)

    @pl.when(has_down)
    def _():
        pl.semaphore_signal(barrier, inc=1, device_id={"seq": s - 2}, device_id_type=MESH)

    pl.semaphore_wait(barrier, size - 1 + jnp.minimum(s // 2, 1) + jnp.minimum((seqs - 1 - s) // 2, 1))

    kinds = 3 + 2 * pairs

    def entry(kind, to, me):
        if kind < 2:
            dst = kvb.at[BACK + me // 2, kind, at(lax.rem(me, 2), rows), :]
            return (k_ref, v_ref)[kind].at[:, at(to, hd)], dst
        if kind == 2:
            return stl.at[to], stb.at[:, at(me, rows)]
        pair, which = (kind - 3) // 2, (kind - 3) % 2
        src = (q_ref, e_ref)[which].at[:, at(to * pairs + pair, pcols)]
        return src, (qb, eb)[which].at[at(me, rows), pl.ds(pair * pcols, pcols)]

    def entry_copy(kind, to):
        src, dst = entry(kind, to, p)
        return pltpu.make_async_remote_copy(
            src_ref=src, dst_ref=dst, send_sem=in_s.at[kind, to], recv_sem=in_r.at[kind, p],
            device_id=dev(to), device_id_type=MESH)

    def entry_got(kind, by):
        _, dst = entry(kind, p, flip(p, by))
        pltpu.make_async_remote_copy(
            src_ref=dst, dst_ref=dst, send_sem=in_s.at[kind, flip(p, by)], recv_sem=in_r.at[kind, flip(p, by)],
            device_id=dev(flip(p, by)), device_id_type=MESH).wait_recv()

    def entry_own(kind):
        src, dst = entry(kind, p, p)
        return pltpu.make_async_copy(src, dst, loc_sem.at[kind])

    order = tuple(sorted(range(1, size), key=lambda by: (by // 2 > 0, by // 2 == 3, by % 2, by)))

    for kind in (0, 1) + tuple(range(3, kinds)):
        entry_own(kind).start()
    for by in order:
        for kind in (0, 1):
            entry_copy(kind, flip(p, by)).start()

    lane = lax.broadcasted_iota(jnp.int32, (rows, hd), 1)
    delta = jnp.zeros((rows, hd), f32)
    for head in range(width * size):
        here = pl.ds(head * hd, hd)
        one = jnp.sum(e_ref[:, here].astype(f32) * o_ref[:, here].astype(f32), axis=1, keepdims=True)
        delta = jnp.where(lane == head, one, delta)
    delta = delta.T
    for to in range(size):
        stl[to, :width, :] = lse_ref[to * width : (to + 1) * width, :] * LOG2E
        stl[to, width:, :] = delta[to * width : (to + 1) * width, :]
    entry_own(2).start()
    for by in order:
        entry_copy(2, flip(p, by)).start()
    for kind in range(3, kinds):
        entry_copy(kind, flip(p, 1)).start()
    for pair in range(pairs):
        for by in order[1:]:
            for which in range(2):
                entry_copy(3 + 2 * pair + which, flip(p, by)).start()

    first = plane * size - BACK * 2
    for a in range(2 * window):
        row = seg_ref[pl.ds(jnp.maximum(first + a, 0), 1), :].astype(f32)
        segk[a * rows : (a + 1) * rows, :] = jnp.broadcast_to(row, (rows, hd)).T
        if a >= 2 * BACK:
            segq[:, (a - 2 * BACK) * rows : (a - 2 * BACK + 1) * rows] = row
    dqt[...] = jnp.zeros_like(dqt)
    acck[...] = jnp.zeros_like(acck)
    accv[...] = jnp.zeros_like(accv)

    def hand(w):
        return pltpu.make_async_remote_copy(
            src_ref=kvb.at[w + tiles], dst_ref=kvb.at[w], send_sem=fw_s.at[w], recv_sem=fw_r.at[w],
            device_id={"seq": s + 2}, device_id_type=MESH)

    def back(w):
        return pltpu.make_async_remote_copy(
            src_ref=ps.at[w], dst_ref=pr.at[w], send_sem=pt_s.at[w], recv_sem=pt_r.at[w],
            device_id={"seq": s - 2}, device_id_type=MESH)

    row_at = lax.broadcasted_iota(jnp.int32, (tile, tile), 0)
    col_at = lax.broadcasted_iota(jnp.int32, (tile, tile), 1)

    def work(i, w, pair):
        q_rows = at(i, tile)
        key, val = kvb[w, 0], kvb[w, 1]
        key_t = key.T
        k_seg = segk[at(w, tile), :]
        allowed = jnp.concatenate([k_seg] * (tile // hd), axis=1) == segq[:, q_rows]
        if not isinstance(w, int) or w >= BACK:
            allowed &= row_at + (w - BACK - i) * tile <= col_at
        mine = range(pair * width // pairs, (pair + 1) * width // pairs)
        queries = [qb[q_rows, m * hd : (m + 1) * hd] for m in mine]
        grads = [eb[q_rows, m * hd : (m + 1) * hd] for m in mine]
        scores = [dot_nt(key, query) for query in queries]
        dprobs = [dot_nt(val, grad) for grad in grads]
        low, dscores = [], []
        for m, score, dprob in zip(mine, scores, dprobs):
            lse = stb[m : m + 1, q_rows]
            delta = stb[width + m : width + m + 1, q_rows]
            probs = jnp.exp2(jnp.where(allowed, score * (scale * LOG2E) - lse, -jnp.inf))
            low.append(probs.astype(bf16))
            dscores.append((probs * (dprob - delta)).astype(bf16))
        accv[w] += dot(jnp.concatenate(low, axis=1), jnp.concatenate(grads, axis=0))
        acck[w] += dot(jnp.concatenate(dscores, axis=1), jnp.concatenate(queries, axis=0))
        for m, dscore in zip(mine, dscores):
            dqt[i, m] += dot(key_t, dscore)

    def leave(which, to, me):
        if which < pairs:
            src = dqs.at[at(to, rows), pl.ds(which * pcols, pcols)]
            return src, dq_out.at[:, at(me * pairs + which, pcols)]
        src, dst = ((dks, dk_out), (dvs, dv_out))[which - pairs]
        return src.at[at(to, rows), :], dst.at[:, at(me, hd)]

    leaves = pairs + 2

    def leave_copy(which, to):
        src, dst = leave(which, to, p)
        return pltpu.make_async_remote_copy(
            src_ref=src, dst_ref=dst, send_sem=out_s.at[which, to], recv_sem=out_r.at[which, p],
            device_id=dev(to), device_id_type=MESH)

    def leave_got(which, by):
        _, dst = leave(which, p, flip(p, by))
        pltpu.make_async_remote_copy(
            src_ref=dst, dst_ref=dst, send_sem=out_s.at[which, flip(p, by)], recv_sem=out_r.at[which, flip(p, by)],
            device_id=dev(flip(p, by)), device_id_type=MESH).wait_recv()

    def leave_own(which):
        src, dst = leave(which, p, p)
        return pltpu.make_async_copy(src, dst, loc_sem.at[kinds + which])

    def leave_start(which, i):
        for b in range(2):
            to = 2 * i + b

            @pl.when(to != p)
            def _():
                leave_copy(which, to).start()

            @pl.when(to == p)
            def _():
                leave_own(which).start()

    def leave_query(i, pair):
        for m in range(pair * width // pairs, (pair + 1) * width // pairs):
            dqs[at(i, tile), m * hd : (m + 1) * hd] = (dqt[i, m] * scale).T.astype(bf16)
        leave_start(pair, i)

    entry_own(2).wait()
    for kind in range(2, kinds):
        if kind > 2:
            entry_own(kind).wait()
    entry_own(0).wait()
    entry_own(1).wait()
    for j in range(tiles):
        for by in range(max(2 * j, 1), 2 * j + 2):
            entry_got(0, by)
            entry_got(1, by)
        t = flip(own, j)

        @pl.when(has_up)
        def _():
            hand(t + BACK - tiles).start()

        if j == 0:
            for kind in range(2, kinds):
                entry_got(kind, 1)

        @pl.when(t <= own)
        def _():
            for pair in range(pairs):
                work(own, t + BACK, pair)

    for j in range(1, tiles):
        for by in range(2 * j, 2 * j + 2):
            for kind in (2, 3, 4):
                entry_got(kind, by)
        i = flip(own, j)

        @pl.loop(0, i + 1)
        def _(t):
            work(i, t + BACK, 0)

    @pl.when(has_down)
    def _():
        for w in range(BACK - 1, BACK - tiles - 1, -1):
            hand(w).wait_recv()
            if w >= tiles:
                @pl.when(has_up)
                def _():
                    hand(w - tiles).start()

            @pl.loop(0, min(tiles - 1, w) + 1)
            def _(i):
                work(i, w, 0)

            @pl.when(own <= w)
            def _():
                for pair in range(1, pairs):
                    work(own, w, pair)

    for i in range(BACK - tiles, tiles):
        leave_query(i, 0)

    @pl.when(has_two)
    def _():
        for w in range(BACK - tiles - 1, -1, -1):
            hand(w).wait_recv()

            @pl.loop(0, w + 1)
            def _(i):
                work(i, w, 0)

            @pl.when(own <= w)
            def _():
                for pair in range(1, pairs):
                    work(own, w, pair)

    for i in range(BACK - tiles):
        leave_query(i, 0)
    for pair in range(1, pairs):
        leave_query(own, pair)

    for j in range(1, tiles):
        for by in range(2 * j, 2 * j + 2):
            for kind in range(5, kinds):
                entry_got(kind, by)

    def rest(w):
        @pl.loop(max(w - BACK, 0), min(tiles - 1, w) + 1)
        def _(i):
            @pl.when(i != own)
            def _():
                for pair in range(1, pairs):
                    work(i, w, pair)

    def put(w):
        ps[w, 0] = acck[w].astype(bf16)
        ps[w, 1] = accv[w].astype(bf16)
        back(w).start()

    def join(w):
        back(w - tiles).wait_recv()
        acck[w] += pr[w - tiles, 0].astype(f32)
        accv[w] += pr[w - tiles, 1].astype(f32)

    @pl.when(has_two)
    def _():
        for w in range(BACK - tiles):
            rest(w)
            put(w)

    @pl.when(has_down)
    def _():
        for w in range(BACK - tiles, BACK):
            rest(w)
            if w < tiles:
                put(w)

    for w in range(BACK, window):
        rest(w)
        for pair in range(1, pairs):
            @pl.when(w - BACK != own)
            def _():
                leave_query(w - BACK, pair)

    @pl.when(has_down)
    def _():
        for w in range(tiles, BACK):
            @pl.when(has_up)
            def _():
                join(w)

            put(w)

    for w in range(BACK, window):
        @pl.when(has_up)
        def _():
            join(w)

        t = w - BACK
        dks[t * tile : (t + 1) * tile, :] = (acck[w] * scale).astype(bf16)
        dvs[t * tile : (t + 1) * tile, :] = accv[w].astype(bf16)
        leave_start(pairs, t)
        leave_start(pairs + 1, t)

    for which in range(leaves):
        leave_own(which).wait()
        for by in range(1, size):
            leave_got(which, by)
            leave_copy(which, flip(p, by)).wait_send()
    for kind in range(kinds):
        for by in range(1, size):
            entry_copy(kind, flip(p, by)).wait_send()
    for w in range(BACK):
        low = w < BACK - tiles

        @pl.when(has_up & has_down if low else has_up)
        def _():
            hand(w).wait_send()

        @pl.when(has_two if low else has_down)
        def _():
            back(w).wait_send()


def shards(query, key, value, out, output_gradient, log_sum_exp, segment_ids):
    n, seqs = lax.axis_size("head"), lax.axis_size("seq")
    hd = HEAD_SIZE
    rows = query.shape[0]
    size = 2 * n
    cols = query.shape[1] // size
    width = cols // hd
    pairs = width // 2
    tile, tiles = 2 * rows, size // 2
    window = tiles + BACK
    bf16, f32 = jnp.bfloat16, jnp.float32
    kinds, leaves = 3 + 2 * pairs, pairs + 2
    vmem = pl.BlockSpec(memory_space=pltpu.VMEM)
    dma = pltpu.SemaphoreType.DMA
    return pl.pallas_call(
        functools.partial(kernel, n, seqs, width),
        out_shape=[
            jax.ShapeDtypeStruct(query.shape, bf16),
            jax.ShapeDtypeStruct(key.shape, bf16),
            jax.ShapeDtypeStruct(value.shape, bf16),
        ],
        in_specs=[vmem] * 7,
        out_specs=[vmem] * 3,
        scratch_shapes=[
            pltpu.VMEM((size * rows, cols), bf16),
            pltpu.VMEM((size * rows, cols), bf16),
            pltpu.VMEM((size, 2 * width, rows), f32),
            pltpu.VMEM((2 * width, size * rows), f32),
            pltpu.VMEM((window, 2, tile, hd), bf16),
            pltpu.VMEM((window * tile, hd), f32),
            pltpu.VMEM((1, size * rows), f32),
            pltpu.VMEM((tiles, width, hd, tile), f32),
            pltpu.VMEM((window, tile, hd), f32),
            pltpu.VMEM((window, tile, hd), f32),
            pltpu.VMEM((BACK, 2, tile, hd), bf16),
            pltpu.VMEM((BACK, 2, tile, hd), bf16),
            pltpu.VMEM((size * rows, cols), bf16),
            pltpu.VMEM((size * rows, hd), bf16),
            pltpu.VMEM((size * rows, hd), bf16),
            dma((kinds + leaves,)),
            dma((kinds, size)),
            dma((kinds, size)),
            dma((BACK,)),
            dma((BACK,)),
            dma((BACK,)),
            dma((BACK,)),
            dma((leaves, size)),
            dma((leaves, size)),
        ],
        compiler_params=pltpu.CompilerParams(collective_id=0, has_side_effects=True),
    )(query, output_gradient, out, key, value, log_sum_exp.T, segment_ids.reshape(-1, hd))


def solution(mesh):
    placed = (P(("seq", "head"), None),) * 6 + (P(),)
    return jax.shard_map(
        lambda *a: tuple(shards(*a)),
        mesh=mesh,
        in_specs=placed,
        out_specs=(P(("seq", "head"), None),) * 3,
        check_vma=False,
    )
```

time: 85.2 us -> 70.5 us (0.83)
  the two profiles are of different devices: /device:TPU:13 before, /device:TPU:23 now
where the time goes in v1:
time: 70.5 us; the launch traced here: 70.3 us
  Pallas kernels  65.5 us (93%)
  local copies, waits for them, and re-layouts  4.08 us (6%)
    pallas_call x1, Pallas kernels, shards(): pl.pallas_call(functools.partial(kernel, n, seqs, width), out_shape=[jax....  65.5 us
    unnamed x7, local copies, waits for them, and re-layouts  4.08 us

profile of v1, /device:TPU:23, one launch (start us, length us, event | category | flops | bytes accessed | tf_op | source)
XLA Modules:
  0.0 70.3 jit_solution(12456155918730685781)
XLA Ops:
  0.6 65.5 %shard_map.94 = (bf16[128,4096]{1,0:T(8,128)(2,1)}, bf16[128,1024]{1,0:T(8,128)(2,1)}, bf16[128,1024]{1,0:T(8,128)(2,1)}) custom-call(bf16[128,4096]{1,0:T(8,128)(2,1)} %q_ref.1, bf16[128,4096]{1,0:T(8,128)(2,1)} %e_ref.1, bf16[128,4096]{1,0:T(8,128)(2,1)} %o_ref.1, bf16[128,1024]{1,0:T(8,128)(2,1)} %k_ref.1, bf16[128,1024]{1,0:T(8,128)(2,1)} %v_ref.1, ...), custom_call_target="tpu_custom_call" | custom-call | tf_op jit(solution)/shard_map/pallas_call | solution.py:398
  66.2 0.0 copy-start.1
  66.2 2.3 %copy.13 = bf16[128,4096]{1,0:T(8,128)(2,1)} copy(bf16[128,4096]{1,0:T(8,128)(2,1)} %get-tuple-element.6) | data formatting | bytes 2097152
  68.5 0.0 copy-done.1
  68.5 0.0 copy-start
  68.5 0.7 copy.14
  69.2 0.3 copy-done
  69.6 0.7 copy.15
Async XLA Ops:
  66.2 2.3 %copy-start.1 = (bf16[128,1024]{1,0:T(8,128)(2,1)S(1)}, bf16[128,1024]{1,0:T(8,128)(2,1)}, u32[]{:S(2)}) copy-start(bf16[128,1024]{1,0:T(8,128)(2,1)} %get-tuple-element.7) | copy-start | bytes 786436
  68.5 1.0 %copy-start = (bf16[128,1024]{1,0:T(8,128)(2,1)S(1)}, bf16[128,1024]{1,0:T(8,128)(2,1)}, u32[]{:S(2)}) copy-start(bf16[128,1024]{1,0:T(8,128)(2,1)} %get-tuple-element.8) | copy-start | bytes 786436

commit v2 on v1

--- a/solution.py
+++ b/solution.py
@@ -25,15 +25,21 @@
 
 def kernel(
     n, seqs, width,
-    q_ref, e_ref, o_ref, k_ref, v_ref, lse_ref, seg_ref,
+    q_in, e_in, o_in, k_in, v_in, lse_ref, seg_ref,
     dq_out, dk_out, dv_out,
-    qb, eb, stl, stb, kvb, segk, segq, dqt, acck, accv, ps, pr, dqs, dks, dvs,
+    k_ref, v_ref, e_ref, o_ref, q_ref, load_sem, qb, eb, stl, stb, kvb, segk, segq, dqt, acck, accv, ps, pr, dqs, dks, dvs,
     loc_sem, in_s, in_r, fw_s, fw_r, pt_s, pt_r, out_s, out_r,
 ):
     s = lax.axis_index("seq")
     h = lax.axis_index("head")
     rows = q_ref.shape[0]
     hd = HEAD_SIZE
+    loads = [
+        pltpu.make_async_copy(src, dst, load_sem.at[at])
+        for at, (src, dst) in enumerate(((k_in, k_ref), (v_in, v_ref), (e_in, e_ref), (o_in, o_ref), (q_in, q_ref)))
+    ]
+    for load in loads:
+        load.start()
     tile = 2 * rows
     size = 2 * n
     tiles = size // 2
@@ -107,11 +113,14 @@
 
     order = tuple(sorted(range(1, size), key=lambda by: (by // 2 > 0, by // 2 == 3, by % 2, by)))
 
-    for kind in (0, 1) + tuple(range(3, kinds)):
+    for kind in (0, 1):
+        loads[kind].wait()
         entry_own(kind).start()
     for by in order:
         for kind in (0, 1):
             entry_copy(kind, flip(p, by)).start()
+    loads[2].wait()
+    loads[3].wait()
 
     lane = lax.broadcasted_iota(jnp.int32, (rows, hd), 1)
     delta = jnp.zeros((rows, hd), f32)
@@ -126,12 +135,14 @@
     entry_own(2).start()
     for by in order:
         entry_copy(2, flip(p, by)).start()
+    loads[4].wait()
     for kind in range(3, kinds):
+        entry_own(kind).start()
         entry_copy(kind, flip(p, 1)).start()
-    for pair in range(pairs):
-        for by in order[1:]:
-            for which in range(2):
-                entry_copy(3 + 2 * pair + which, flip(p, by)).start()
+    for near in (order[1:5], order[5:]):
+        for kind in range(3, kinds):
+            for by in near:
+                entry_copy(kind, flip(p, by)).start()
 
     first = plane * size - BACK * 2
     for a in range(2 * window):
@@ -218,17 +229,31 @@
             def _():
                 leave_own(which).start()
 
-    def leave_query(i, pair):
-        for m in range(pair * width // pairs, (pair + 1) * width // pairs):
+    def fill(i):
+        for m in range(width):
             dqs[at(i, tile), m * hd : (m + 1) * hd] = (dqt[i, m] * scale).T.astype(bf16)
-        leave_start(pair, i)
-
-    entry_own(2).wait()
-    for kind in range(2, kinds):
-        if kind > 2:
-            entry_own(kind).wait()
-    entry_own(0).wait()
-    entry_own(1).wait()
+
+    def all_pairs(i, w):
+        for pair in range(pairs):
+            work(i, w, pair)
+
+    def query_got(j, pair):
+        for by in range(2 * j, 2 * j + 2):
+            for kind in ((2,) if pair == 0 else ()) + (3 + 2 * pair, 4 + 2 * pair):
+                entry_got(kind, by)
+
+    def put(w):
+        ps[w, 0] = acck[w].astype(bf16)
+        ps[w, 1] = accv[w].astype(bf16)
+        back(w).start()
+
+    def join(w):
+        back(w - tiles).wait_recv()
+        acck[w] += pr[w - tiles, 0].astype(f32)
+        accv[w] += pr[w - tiles, 1].astype(f32)
+
+    for kind in range(kinds):
+        entry_own(kind).wait()
     for j in range(tiles):
         for by in range(max(2 * j, 1), 2 * j + 2):
             entry_got(0, by)
@@ -245,39 +270,51 @@
 
         @pl.when(t <= own)
         def _():
-            for pair in range(pairs):
-                work(own, t + BACK, pair)
-
-    for j in range(1, tiles):
-        for by in range(2 * j, 2 * j + 2):
-            for kind in (2, 3, 4):
-                entry_got(kind, by)
-        i = flip(own, j)
-
-        @pl.loop(0, i + 1)
-        def _(t):
-            work(i, t + BACK, 0)
-
-    @pl.when(has_down)
-    def _():
-        for w in range(BACK - 1, BACK - tiles - 1, -1):
+            all_pairs(own, t + BACK)
+
+    last = tiles - 1
+    far = flip(own, last)
+
+    def before(j):
+        w = BACK - tiles + flip(own, j)
+
+        @pl.when(has_down)
+        def _():
             hand(w).wait_recv()
-            if w >= tiles:
-                @pl.when(has_up)
-                def _():
-                    hand(w - tiles).start()
-
-            @pl.loop(0, min(tiles - 1, w) + 1)
-            def _(i):
-                work(i, w, 0)
+
+            @pl.when(has_up & (w >= tiles))
+            def _():
+                hand(w - tiles).start()
 
             @pl.when(own <= w)
             def _():
-                for pair in range(1, pairs):
-                    work(own, w, pair)
-
-    for i in range(BACK - tiles, tiles):
-        leave_query(i, 0)
+                all_pairs(own, w)
+
+    def near(w, pair):
+        @pl.loop(0, min(tiles - 1, w) + 1)
+        def _(i):
+            @pl.when((i != far) & (i != own))
+            def _():
+                work(i, w, pair)
+
+    for j in range(last):
+        before(j)
+    for pair in range(pairs):
+        for j in range(1, last):
+            query_got(j, pair)
+            i = flip(own, j)
+
+            @pl.loop(0, i + 1)
+            def _(t):
+                work(i, t + BACK, pair)
+
+        if pair == 0:
+            before(last)
+
+        @pl.when(has_down)
+        def _():
+            for w in range(BACK - tiles, BACK):
+                near(w, pair)
 
     @pl.when(has_two)
     def _():
@@ -286,60 +323,59 @@
 
             @pl.loop(0, w + 1)
             def _(i):
-                work(i, w, 0)
-
-            @pl.when(own <= w)
-            def _():
-                for pair in range(1, pairs):
-                    work(own, w, pair)
-
-    for i in range(BACK - tiles):
-        leave_query(i, 0)
-    for pair in range(1, pairs):
-        leave_query(own, pair)
-
-    for j in range(1, tiles):
-        for by in range(2 * j, 2 * j + 2):
-            for kind in range(5, kinds):
-                entry_got(kind, by)
-
-    def rest(w):
-        @pl.loop(max(w - BACK, 0), min(tiles - 1, w) + 1)
-        def _(i):
-            @pl.when(i != own)
-            def _():
-                for pair in range(1, pairs):
-                    work(i, w, pair)
-
-    def put(w):
-        ps[w, 0] = acck[w].astype(bf16)
-        ps[w, 1] = accv[w].astype(bf16)
-        back(w).start()
-
-    def join(w):
-        back(w - tiles).wait_recv()
-        acck[w] += pr[w - tiles, 0].astype(f32)
-        accv[w] += pr[w - tiles, 1].astype(f32)
-
-    @pl.when(has_two)
-    def _():
-        for w in range(BACK - tiles):
-            rest(w)
-            put(w)
-
-    @pl.when(has_down)
-    def _():
-        for w in range(BACK - tiles, BACK):
-            rest(w)
-            if w < tiles:
+                @pl.when(i != far)
+                def _():
+                    all_pairs(i, w)
+
+    bottom = jnp.maximum(far, jnp.maximum(BACK - tiles * plane, 0))
+    for pair in range(pairs - 1):
+        query_got(last, pair)
+
+        @pl.loop(bottom, far + BACK + 1)
+        def _(w):
+            work(far, w, pair)
+
+    def rest(w, late):
+        if late:
+            @pl.when(far <= w)
+            def _():
+                work(far, w, pairs - 1)
+                if w < tiles:
+                    put(w)
+        elif w < last:
+            @pl.when(far > w)
+            def _():
                 put(w)
 
-    for w in range(BACK, window):
-        rest(w)
-        for pair in range(1, pairs):
-            @pl.when(w - BACK != own)
-            def _():
-                leave_query(w - BACK, pair)
+    def carry(late):
+        @pl.when(has_two)
+        def _():
+            for w in range(BACK - tiles):
+                rest(w, late)
+
+        @pl.when(has_down)
+        def _():
+            for w in range(BACK - tiles, BACK):
+                rest(w, late)
+
+    carry(False)
+    for j in range(last):
+        fill(flip(own, j))
+    query_got(last, pairs - 1)
+    for j in range(1, last):
+        for pair in range(pairs):
+            leave_start(pair, flip(own, j))
+    carry(True)
+    for pair in range(pairs):
+        leave_start(pair, own)
+
+    @pl.loop(0, far + 1)
+    def _(t):
+        work(far, t + BACK, pairs - 1)
+
+    fill(far)
+    for pair in range(pairs):
+        leave_start(pair, far)
 
     @pl.when(has_down)
     def _():
@@ -379,6 +415,21 @@
         @pl.when(has_two if low else has_down)
         def _():
             back(w).wait_send()
+
+
+def move(*refs):
+    count = (len(refs) - 2) // 3
+    ins, outs, held = refs[:count], refs[count : 2 * count], refs[2 * count : 3 * count]
+    in_sem, out_sem = refs[3 * count :]
+    reads = [pltpu.make_async_copy(a, b, in_sem.at[at]) for at, (a, b) in enumerate(zip(ins, held))]
+    writes = [pltpu.make_async_copy(a, b, out_sem.at[at]) for at, (a, b) in enumerate(zip(held, outs))]
+    for read in reads:
+        read.start()
+    for read, write in zip(reads, writes):
+        read.wait()
+        write.start()
+    for write in writes:
+        write.wait()
 
 
 def shards(query, key, value, out, output_gradient, log_sum_exp, segment_ids):
@@ -395,16 +446,23 @@
     kinds, leaves = 3 + 2 * pairs, pairs + 2
     vmem = pl.BlockSpec(memory_space=pltpu.VMEM)
     dma = pltpu.SemaphoreType.DMA
-    return pl.pallas_call(
+    anywhere = pl.BlockSpec(memory_space=pl.ANY)
+    parts = pl.pallas_call(
         functools.partial(kernel, n, seqs, width),
         out_shape=[
             jax.ShapeDtypeStruct(query.shape, bf16),
             jax.ShapeDtypeStruct(key.shape, bf16),
             jax.ShapeDtypeStruct(value.shape, bf16),
         ],
-        in_specs=[vmem] * 7,
-        out_specs=[vmem] * 3,
+        in_specs=[anywhere] * 5 + [vmem] * 2,
+        out_specs=[anywhere] * 3,
         scratch_shapes=[
+            pltpu.VMEM(key.shape, bf16),
+            pltpu.VMEM(value.shape, bf16),
+            pltpu.VMEM(query.shape, bf16),
+            pltpu.VMEM(query.shape, bf16),
+            pltpu.VMEM(query.shape, bf16),
+            dma((5,)),
             pltpu.VMEM((size * rows, cols), bf16),
             pltpu.VMEM((size * rows, cols), bf16),
             pltpu.VMEM((size, 2 * width, rows), f32),
@@ -432,6 +490,13 @@
         ],
         compiler_params=pltpu.CompilerParams(collective_id=0, has_side_effects=True),
     )(query, output_gradient, out, key, value, log_sum_exp.T, segment_ids.reshape(-1, hd))
+    return pl.pallas_call(
+        move,
+        out_shape=[jax.ShapeDtypeStruct(part.shape, bf16) for part in parts],
+        in_specs=[anywhere] * 3,
+        out_specs=[anywhere] * 3,
+        scratch_shapes=[pltpu.VMEM(part.shape, bf16) for part in parts] + [dma((3,)), dma((3,))],
+    )(*parts)
 
 
 def solution(mesh):

time: 70.5 us -> 65.9 us (0.935)
  local copies, waits for them, and re-layouts: 4.08 us -> 0 us
  Pallas kernels: 65.5 us -> 64.7 us
    unnamed x7 -> x0, local copies, waits for them, and re-layouts: 4.08 us -> none
    pallas_call x1, Pallas kernels: 65.5 us -> 62.3 us  [shards(): pl.pallas_call(functools.partial(kernel, n, seqs, width), out_shape=[jax....]
    pallas_call x0 -> x1, Pallas kernels: none -> 2.41 us  [shards(): pl.pallas_call(move, out_shape=[jax.ShapeDtypeStruct(part.shape, bf16) fo...]
where the time goes in v2:
time: 65.9 us; the launch traced here: 65.5 us
  Pallas kernels  64.7 us (98%)
  between operations  0.8 us (1%)
    pallas_call x1, Pallas kernels, shards(): pl.pallas_call(functools.partial(kernel, n, seqs, width), out_shape=[jax....  62.3 us
    pallas_call x1, Pallas kernels, shards(): pl.pallas_call(move, out_shape=[jax.ShapeDtypeStruct(part.shape, bf16) fo...  2.41 us

profile of v2, /device:TPU:23, one launch (start us, length us, event | category | flops | bytes accessed | tf_op | source)
XLA Modules:
  0.0 65.5 jit_solution(15358321193060493096)
XLA Ops:
  0.6 62.3 %shard_map.94 = (bf16[128,4096]{1,0:T(8,128)(2,1)}, bf16[128,1024]{1,0:T(8,128)(2,1)}, bf16[128,1024]{1,0:T(8,128)(2,1)}) custom-call(bf16[128,4096]{1,0:T(8,128)(2,1)} %q_in.1, bf16[128,4096]{1,0:T(8,128)(2,1)} %e_in.1, bf16[128,4096]{1,0:T(8,128)(2,1)} %o_in.1, bf16[128,1024]{1,0:T(8,128)(2,1)} %k_in.1, bf16[128,1024]{1,0:T(8,128)(2,1)} %v_in.1, ...), custom_call_target="tpu_custom_call" | custom-call | tf_op jit(solution)/shard_map/pallas_call | solution.py:450
  63.0 2.4 %shard_map.95 = (bf16[128,4096]{1,0:T(8,128)(2,1)}, bf16[128,1024]{1,0:T(8,128)(2,1)}, bf16[128,1024]{1,0:T(8,128)(2,1)}) custom-call(bf16[128,4096]{1,0:T(8,128)(2,1)} %get-tuple-element.6.refs_0_, bf16[128,1024]{1,0:T(8,128)(2,1)} %get-tuple-element.7.refs_1_, bf16[128,1024]{1,0:T(8,128)(2,1)} %get-tuple-element.8.refs_2_), custom_call_target="tpu_custom_call" | custom-call | tf_op jit(solution)/shard_map/pallas_call | solution.py:493

commit v3 on v2

--- a/solution.py
+++ b/solution.py
@@ -233,6 +233,18 @@
         for m in range(width):
             dqs[at(i, tile), m * hd : (m + 1) * hd] = (dqt[i, m] * scale).T.astype(bf16)
 
+    def by_twos(i, start, stop, pair):
+        count = stop - start
+
+        @pl.loop(0, count // 2)
+        def _(t):
+            work(i, start + 2 * t, pair)
+            work(i, start + 2 * t + 1, pair)
+
+        @pl.when(lax.rem(count, 2) == 1)
+        def _():
+            work(i, stop - 1, pair)
+
     def all_pairs(i, w):
         for pair in range(pairs):
             work(i, w, pair)
@@ -290,12 +302,16 @@
             def _():
                 all_pairs(own, w)
 
+    sides = [flip(own, j) for j in range(1, last)]
+
     def near(w, pair):
-        @pl.loop(0, min(tiles - 1, w) + 1)
-        def _(i):
-            @pl.when((i != far) & (i != own))
-            def _():
+        for i in sides:
+            if w >= tiles - 1:
                 work(i, w, pair)
+            else:
+                @pl.when(i <= w)
+                def _():
+                    work(i, w, pair)
 
     for j in range(last):
         before(j)
@@ -303,10 +319,7 @@
         for j in range(1, last):
             query_got(j, pair)
             i = flip(own, j)
-
-            @pl.loop(0, i + 1)
-            def _(t):
-                work(i, t + BACK, pair)
+            by_twos(i, BACK, i + BACK + 1, pair)
 
         if pair == 0:
             before(last)
@@ -327,73 +340,85 @@
                 def _():
                     all_pairs(i, w)
 
+    for j in range(last):
+        fill(flip(own, j))
+
+    for w in range(last):
+        @pl.when((has_two if w < BACK - tiles else has_down) & (far > w))
+        def _():
+            put(w)
+
     bottom = jnp.maximum(far, jnp.maximum(BACK - tiles * plane, 0))
     for pair in range(pairs - 1):
         query_got(last, pair)
-
-        @pl.loop(bottom, far + BACK + 1)
-        def _(w):
-            work(far, w, pair)
-
-    def rest(w, late):
-        if late:
-            @pl.when(far <= w)
-            def _():
-                work(far, w, pairs - 1)
-                if w < tiles:
-                    put(w)
-        elif w < last:
-            @pl.when(far > w)
-            def _():
-                put(w)
-
-    def carry(late):
-        @pl.when(has_two)
-        def _():
-            for w in range(BACK - tiles):
-                rest(w, late)
-
-        @pl.when(has_down)
-        def _():
-            for w in range(BACK - tiles, BACK):
-                rest(w, late)
-
-    carry(False)
-    for j in range(last):
-        fill(flip(own, j))
+        by_twos(far, bottom, far + BACK + 1, pair)
     query_got(last, pairs - 1)
     for j in range(1, last):
         for pair in range(pairs):
             leave_start(pair, flip(own, j))
-    carry(True)
+
+    def rest(*some):
+        for w in some:
+            work(far, w, pairs - 1)
+        for w in some:
+            @pl.when(w < tiles)
+            def _():
+                put(w)
+
+    @pl.when(has_two)
+    def _():
+        for w in range(0, BACK - tiles, 2):
+            @pl.when(far <= w)
+            def _():
+                rest(w, w + 1)
+
+            @pl.when(far == w + 1)
+            def _():
+                rest(w + 1)
+
+    turns = tuple(range(tiles - 1, -1, -1))
+    ws = [BACK - tiles + flip(own, j) for j in turns]
+
+    @pl.when(has_down)
+    def _():
+        rest(*ws[:2])
+
+        @pl.when(far <= ws[3])
+        def _():
+            rest(*ws[2:])
+
+        @pl.when(far > ws[3])
+        def _():
+            rest(ws[2])
+
     for pair in range(pairs):
         leave_start(pair, own)
-
-    @pl.loop(0, far + 1)
-    def _(t):
-        work(far, t + BACK, pairs - 1)
-
+    by_twos(far, BACK, far + BACK + 1, pairs - 1)
     fill(far)
     for pair in range(pairs):
         leave_start(pair, far)
 
     @pl.when(has_down)
     def _():
-        for w in range(tiles, BACK):
-            @pl.when(has_up)
-            def _():
-                join(w)
-
-            put(w)
-
-    for w in range(BACK, window):
+        for w in ws:
+            @pl.when(w >= tiles)
+            def _():
+                @pl.when(has_up)
+                def _():
+                    join(w)
+
+                put(w)
+
+    for j in turns:
+        t = flip(own, j)
+        w = t + BACK
+
         @pl.when(has_up)
         def _():
             join(w)
 
-        t = w - BACK
-        dks[t * tile : (t + 1) * tile, :] = (acck[w] * scale).astype(bf16)
-        dvs[t * tile : (t + 1) * tile, :] = accv[w].astype(bf16)
+        dks[at(t, tile), :] = (acck[w] * scale).astype(bf16)
+        dvs[at(t, tile), :] = accv[w].astype(bf16)
         leave_start(pairs, t)
         leave_start(pairs + 1, t)
 
@@ -418,18 +443,12 @@
 
 
 def move(*refs):
-    count = (len(refs) - 2) // 3
-    ins, outs, held = refs[:count], refs[count : 2 * count], refs[2 * count : 3 * count]
-    in_sem, out_sem = refs[3 * count :]
-    reads = [pltpu.make_async_copy(a, b, in_sem.at[at]) for at, (a, b) in enumerate(zip(ins, held))]
-    writes = [pltpu.make_async_copy(a, b, out_sem.at[at]) for at, (a, b) in enumerate(zip(held, outs))]
-    for read in reads:
-        read.start()
-    for read, write in zip(reads, writes):
-        read.wait()
-        write.start()
-    for write in writes:
-        write.wait()
+    ins, outs, sems = refs[:3], refs[3:6], refs[6]
+    copies = [pltpu.make_async_copy(a, b, sems.at[at]) for at, (a, b) in enumerate(zip(ins, outs))]
+    for copy in copies:
+        copy.start()
+    for copy in copies:
+        copy.wait()
 
 
 def shards(query, key, value, out, output_gradient, log_sum_exp, segment_ids):
@@ -449,13 +468,9 @@
     anywhere = pl.BlockSpec(memory_space=pl.ANY)
     parts = pl.pallas_call(
         functools.partial(kernel, n, seqs, width),
-        out_shape=[
-            jax.ShapeDtypeStruct(query.shape, bf16),
-            jax.ShapeDtypeStruct(key.shape, bf16),
-            jax.ShapeDtypeStruct(value.shape, bf16),
-        ],
+        out_shape=[pltpu.VMEM(like.shape, bf16) for like in (query, key, value)],
         in_specs=[anywhere] * 5 + [vmem] * 2,
-        out_specs=[anywhere] * 3,
+        out_specs=[vmem] * 3,
         scratch_shapes=[
             pltpu.VMEM(key.shape, bf16),
             pltpu.VMEM(value.shape, bf16),
@@ -493,9 +508,10 @@
     return pl.pallas_call(
         move,
         out_shape=[jax.ShapeDtypeStruct(part.shape, bf16) for part in parts],
-        in_specs=[anywhere] * 3,
+        in_specs=[vmem] * 3,
         out_specs=[anywhere] * 3,
-        scratch_shapes=[pltpu.VMEM(part.shape, bf16) for part in parts] + [dma((3,)), dma((3,))],
+        scratch_shapes=[dma((3,))],
+        compiler_params=pltpu.CompilerParams(vmem_limit_bytes=1 << 20),
     )(*parts)
 
 

time: 65.9 us -> 59.7 us (0.906); the launches traced: 65.5 us -> 58.6 us
  Pallas kernels: 64.7 us -> 57.8 us
    pallas_call x1, Pallas kernels: 62.3 us -> 56.6 us  [shards(): pl.pallas_call(functools.partial(kernel, n, seqs, width), out_shape=[pltp...]
    pallas_call x1, Pallas kernels: 2.41 us -> 1.16 us  [shards(): pl.pallas_call(move, out_shape=[jax.ShapeDtypeStruct(part.shape, bf16) fo...]
where the time goes in v3:
time: 59.7 us; the launch traced here: 58.6 us
  Pallas kernels  57.8 us (97%)
  between operations  0.82 us (1%)
    pallas_call x1, Pallas kernels, shards(): pl.pallas_call(functools.partial(kernel, n, seqs, width), out_shape=[pltp...  56.6 us

profile of v3, /device:TPU:23, one launch (start us, length us, event | category | flops | bytes accessed | tf_op | source)
XLA Modules:
  0.0 58.6 jit_solution(15482434768814464492)
XLA Ops:
  0.6 56.6 %shard_map.94 = (bf16[128,4096]{1,0:T(8,128)(2,1)S(1)}, bf16[128,1024]{1,0:T(8,128)(2,1)S(1)}, bf16[128,1024]{1,0:T(8,128)(2,1)S(1)}) custom-call(bf16[128,4096]{1,0:T(8,128)(2,1)} %q_in.1, bf16[128,4096]{1,0:T(8,128)(2,1)} %e_in.1, bf16[128,4096]{1,0:T(8,128)(2,1)} %o_in.1, bf16[128,1024]{1,0:T(8,128)(2,1)} %k_in.1, bf16[128,1024]{1,0:T(8,128)(2,1)} %v_in.1, ...), custom_call_target="tpu_custom_call" | custom-call | tf_op jit(solution)/shard_map/pallas_call | solution.py:469
  57.3 1.2 %shard_map.95 = (bf16[128,4096]{1,0:T(8,128)(2,1)}, bf16[128,1024]{1,0:T(8,128)(2,1)}, bf16[128,1024]{1,0:T(8,128)(2,1)}) custom-call(bf16[128,4096]{1,0:T(8,128)(2,1)S(1)} %get-tuple-element.6.refs_0_, bf16[128,1024]{1,0:T(8,128)(2,1)S(1)} %get-tuple-element.7.refs_1_, bf16[128,1024]{1,0:T(8,128)(2,1)S(1)} %get-tuple-element.8.refs_2_), custom_call_target="tpu_custom_call" | custom-call | tf_op jit(solution)/shard_map/pallas_call | solution.py:508

commit v4 on v3

--- a/solution.py
+++ b/solution.py
@@ -139,10 +139,23 @@
     for kind in range(3, kinds):
         entry_own(kind).start()
         entry_copy(kind, flip(p, 1)).start()
-    for near in (order[1:5], order[5:]):
-        for kind in range(3, kinds):
-            for by in near:
-                entry_copy(kind, flip(p, by)).start()
+    def peer(base, core):
+        chip = flip(p, base)
+        return chip - lax.rem(chip, 2) + core
+
+    for bases, core, pair in (
+        ((2, 4), 1, 0),
+        ((2, 4), 0, 0),
+        ((2, 4), 1, 1),
+        ((6,), 1, 0),
+        ((2, 4), 0, 1),
+        ((6,), 1, 1),
+        ((6,), 0, 0),
+        ((6,), 0, 1),
+    ):
+        for base in bases:
+            for which in range(2):
+                entry_copy(3 + 2 * pair + which, peer(base, core)).start()
 
     first = plane * size - BACK * 2
     for a in range(2 * window):
@@ -229,8 +242,8 @@
             def _():
                 leave_own(which).start()
 
-    def fill(i):
-        for m in range(width):
+    def fill(i, pair):
+        for m in range(pair * width // pairs, (pair + 1) * width // pairs):
             dqs[at(i, tile), m * hd : (m + 1) * hd] = (dqt[i, m] * scale).T.astype(bf16)
 
     def by_twos(i, start, stop, pair):
@@ -319,7 +332,8 @@
         for j in range(1, last):
             query_got(j, pair)
             i = flip(own, j)
-            by_twos(i, BACK, i + BACK + 1, pair)
+            if pair == 0:
+                by_twos(i, BACK, i + BACK + 1, pair)
 
         if pair == 0:
             before(last)
@@ -340,8 +354,10 @@
                 def _():
                     all_pairs(i, w)
 
-    for j in range(last):
-        fill(flip(own, j))
+    for pair in range(pairs):
+        fill(own, pair)
+    for i in sides:
+        fill(i, 0)
 
     for w in range(last):
         @pl.when((has_two if w < BACK - tiles else has_down) & (far > w))
@@ -351,11 +367,10 @@
     bottom = jnp.maximum(far, jnp.maximum(BACK - tiles * plane, 0))
     for pair in range(pairs - 1):
         query_got(last, pair)
-        by_twos(far, bottom, far + BACK + 1, pair)
+        by_twos(far, jnp.minimum(bottom, BACK), BACK, pair)
     query_got(last, pairs - 1)
-    for j in range(1, last):
-        for pair in range(pairs):
-            leave_start(pair, flip(own, j))
+    for i in sides:
+        leave_start(0, i)
 
     def rest(*some):
         for w in some:
@@ -393,9 +408,18 @@
 
     for pair in range(pairs):
         leave_start(pair, own)
-    by_twos(far, BACK, far + BACK + 1, pairs - 1)
-    fill(far)
+    for i in sides:
+        for pair in range(1, pairs):
+            by_twos(i, BACK, i + BACK + 1, pair)
+            fill(i, pair)
+            leave_start(pair, i)
+
+    @pl.loop(BACK, far + BACK + 1)
+    def _(w):
+        all_pairs(far, w)
+
     for pair in range(pairs):
+        fill(far, pair)
         leave_start(pair, far)
 
     @pl.when(has_down)

time: 59.7 us -> 58 us (0.972)
  Pallas kernels: 57.8 us -> 56.2 us
    pallas_call x1, Pallas kernels: 56.6 us -> 55.1 us  [shards(): pl.pallas_call(functools.partial(kernel, n, seqs, width), out_shape=[pltp...]
where the time goes in v4:
time: 58 us; the launch traced here: 57 us
  Pallas kernels  56.2 us (97%)
  between operations  0.8 us (1%)
    pallas_call x1, Pallas kernels, shards(): pl.pallas_call(functools.partial(kernel, n, seqs, width), out_shape=[pltp...  55.1 us
    pallas_call x1, Pallas kernels, shards(): pl.pallas_call(move, out_shape=[jax.ShapeDtypeStruct(part.shape, bf16) fo...  1.16 us

profile of v4, /device:TPU:23, one launch (start us, length us, event | category | flops | bytes accessed | tf_op | source)
XLA Modules:
  0.0 57.0 jit_solution(6693979563534388117)
XLA Ops:
  0.6 55.1 %shard_map.94 = (bf16[128,4096]{1,0:T(8,128)(2,1)S(1)}, bf16[128,1024]{1,0:T(8,128)(2,1)S(1)}, bf16[128,1024]{1,0:T(8,128)(2,1)S(1)}) custom-call(bf16[128,4096]{1,0:T(8,128)(2,1)} %q_in.1, bf16[128,4096]{1,0:T(8,128)(2,1)} %e_in.1, bf16[128,4096]{1,0:T(8,128)(2,1)} %o_in.1, bf16[128,1024]{1,0:T(8,128)(2,1)} %k_in.1, bf16[128,1024]{1,0:T(8,128)(2,1)} %v_in.1, ...), custom_call_target="tpu_custom_call" | custom-call | tf_op jit(solution)/shard_map/pallas_call | solution.py:493
  55.7 1.2 %shard_map.95 = (bf16[128,4096]{1,0:T(8,128)(2,1)}, bf16[128,1024]{1,0:T(8,128)(2,1)}, bf16[128,1024]{1,0:T(8,128)(2,1)}) custom-call(bf16[128,4096]{1,0:T(8,128)(2,1)S(1)} %get-tuple-element.6.refs_0_, bf16[128,1024]{1,0:T(8,128)(2,1)S(1)} %get-tuple-element.7.refs_1_, bf16[128,1024]{1,0:T(8,128)(2,1)S(1)} %get-tuple-element.8.refs_2_), custom_call_target="tpu_custom_call" | custom-call | tf_op jit(solution)/shard_map/pallas_call | solution.py:532

commit v5 on v4

--- a/solution.py
+++ b/solution.py
@@ -25,9 +25,9 @@
 
 def kernel(
     n, seqs, width,
-    q_in, e_in, o_in, k_in, v_in, lse_ref, seg_ref,
+    q_in, e_in, o_in, k_in, v_in, lse_in, seg_in,
     dq_out, dk_out, dv_out,
-    k_ref, v_ref, e_ref, o_ref, q_ref, load_sem, qb, eb, stl, stb, kvb, segk, segq, dqt, acck, accv, ps, pr, dqs, dks, dvs,
+    k_ref, v_ref, e_ref, o_ref, q_ref, lse_ref, seg_ref, load_sem, qb, eb, stl, stb, kvb, segk, segq, dqt, acck, accv, ps, pr, dqs, dks, dvs,
     loc_sem, in_s, in_r, fw_s, fw_r, pt_s, pt_r, out_s, out_r,
 ):
     s = lax.axis_index("seq")
@@ -36,7 +36,9 @@
     hd = HEAD_SIZE
     loads = [
         pltpu.make_async_copy(src, dst, load_sem.at[at])
-        for at, (src, dst) in enumerate(((k_in, k_ref), (v_in, v_ref), (e_in, e_ref), (o_in, o_ref), (q_in, q_ref)))
+        for at, (src, dst) in enumerate((
+            (k_in, k_ref), (v_in, v_ref), (e_in, e_ref), (o_in, o_ref), (q_in, q_ref), (lse_in, lse_ref), (seg_in, seg_ref),
+        ))
     ]
     for load in loads:
         load.start()
@@ -129,6 +131,8 @@
         one = jnp.sum(e_ref[:, here].astype(f32) * o_ref[:, here].astype(f32), axis=1, keepdims=True)
         delta = jnp.where(lane == head, one, delta)
     delta = delta.T
+    loads[5].wait()
+    loads[6].wait()
     for to in range(size):
         stl[to, :width, :] = lse_ref[to * width : (to + 1) * width, :] * LOG2E
         stl[to, width:, :] = delta[to * width : (to + 1) * width, :]
@@ -326,7 +330,7 @@
                 def _():
                     work(i, w, pair)
 
-    for j in range(last):
+    for j in range(last - 1):
         before(j)
     for pair in range(pairs):
         for j in range(1, last):
@@ -336,7 +340,8 @@
                 by_twos(i, BACK, i + BACK + 1, pair)
 
         if pair == 0:
-            before(last)
+            for j in range(last - 1, tiles):
+                before(j)
 
         @pl.when(has_down)
         def _():
@@ -358,6 +363,7 @@
         fill(own, pair)
     for i in sides:
         fill(i, 0)
+        leave_start(0, i)
 
     for w in range(last):
         @pl.when((has_two if w < BACK - tiles else has_down) & (far > w))
@@ -369,8 +375,6 @@
         query_got(last, pair)
         by_twos(far, jnp.minimum(bottom, BACK), BACK, pair)
     query_got(last, pairs - 1)
-    for i in sides:
-        leave_start(0, i)
 
     def rest(*some):
         for w in some:
@@ -493,7 +497,7 @@
     parts = pl.pallas_call(
         functools.partial(kernel, n, seqs, width),
         out_shape=[pltpu.VMEM(like.shape, bf16) for like in (query, key, value)],
-        in_specs=[anywhere] * 5 + [vmem] * 2,
+        in_specs=[anywhere] * 7,
         out_specs=[vmem] * 3,
         scratch_shapes=[
             pltpu.VMEM(key.shape, bf16),
@@ -501,7 +505,9 @@
             pltpu.VMEM(query.shape, bf16),
             pltpu.VMEM(query.shape, bf16),
             pltpu.VMEM(query.shape, bf16),
-            dma((5,)),
+            pltpu.VMEM(log_sum_exp.shape[::-1], f32),
+            pltpu.VMEM((segment_ids.size // hd, hd), jnp.int32),
+            dma((7,)),
             pltpu.VMEM((size * rows, cols), bf16),
             pltpu.VMEM((size * rows, cols), bf16),
             pltpu.VMEM((size, 2 * width, rows), f32),

time: 58 us -> 56.3 us (0.971); the launches traced: 57 us -> 56 us
  Pallas kernels: 56.2 us -> 55.2 us
    pallas_call x1, Pallas kernels: 55.1 us -> 54 us  [shards(): pl.pallas_call(functools.partial(kernel, n, seqs, width), out_shape=[pltp...]
where the time goes in v5:
time: 56.3 us; the launch traced here: 56 us
  Pallas kernels  55.2 us (98%)
  between operations  0.8 us (1%)
    pallas_call x1, Pallas kernels, shards(): pl.pallas_call(functools.partial(kernel, n, seqs, width), out_shape=[pltp...  54 us
    pallas_call x1, Pallas kernels, shards(): pl.pallas_call(move, out_shape=[jax.ShapeDtypeStruct(part.shape, bf16) fo...  1.16 us

profile of v5, /device:TPU:23, one launch (start us, length us, event | category | flops | bytes accessed | tf_op | source)
XLA Modules:
  0.0 56.0 jit_solution(12268951102515808617)
XLA Ops:
  0.6 54.0 %shard_map.94 = (bf16[128,4096]{1,0:T(8,128)(2,1)S(1)}, bf16[128,1024]{1,0:T(8,128)(2,1)S(1)}, bf16[128,1024]{1,0:T(8,128)(2,1)S(1)}) custom-call(bf16[128,4096]{1,0:T(8,128)(2,1)} %q_in.1, bf16[128,4096]{1,0:T(8,128)(2,1)} %e_in.1, bf16[128,4096]{1,0:T(8,128)(2,1)} %o_in.1, bf16[128,1024]{1,0:T(8,128)(2,1)} %k_in.1, bf16[128,1024]{1,0:T(8,128)(2,1)} %v_in.1, ...), custom_call_target="tpu_custom_call" | custom-call | tf_op jit(solution)/shard_map/pallas_call | solution.py:497
  54.7 1.2 %shard_map.95 = (bf16[128,4096]{1,0:T(8,128)(2,1)}, bf16[128,1024]{1,0:T(8,128)(2,1)}, bf16[128,1024]{1,0:T(8,128)(2,1)}) custom-call(bf16[128,4096]{1,0:T(8,128)(2,1)S(1)} %get-tuple-element.6.refs_0_, bf16[128,1024]{1,0:T(8,128)(2,1)S(1)} %get-tuple-element.7.refs_1_, bf16[128,1024]{1,0:T(8,128)(2,1)S(1)} %get-tuple-element.8.refs_2_), custom_call_target="tpu_custom_call" | custom-call | tf_op jit(solution)/shard_map/pallas_call | solution.py:538

commit v6 on v5

--- a/solution.py
+++ b/solution.py
@@ -151,8 +151,8 @@
         ((2, 4), 1, 0),
         ((2, 4), 0, 0),
         ((2, 4), 1, 1),
+        ((2, 4), 0, 1),
         ((6,), 1, 0),
-        ((2, 4), 0, 1),
         ((6,), 1, 1),
         ((6,), 0, 0),
         ((6,), 0, 1),
@@ -365,6 +365,19 @@
         fill(i, 0)
         leave_start(0, i)
 
+    def side_rest():
+        for i in sides:
+            for pair in range(1, pairs):
+                by_twos(i, BACK, i + BACK + 1, pair)
+                fill(i, pair)
+                leave_start(pair, i)
+
+    late_core = lax.rem(p, 2) == 0
+
+    @pl.when(late_core)
+    def _():
+        side_rest()
+
     for w in range(last):
         @pl.when((has_two if w < BACK - tiles else has_down) & (far > w))
         def _():
@@ -412,11 +425,9 @@
 
     for pair in range(pairs):
         leave_start(pair, own)
-    for i in sides:
-        for pair in range(1, pairs):
-            by_twos(i, BACK, i + BACK + 1, pair)
-            fill(i, pair)
-            leave_start(pair, i)
+    @pl.when(jnp.logical_not(late_core))
+    def _():
+        side_rest()
 
     @pl.loop(BACK, far + BACK + 1)
     def _(w):

time: 56.3 us -> 56.2 us (level); the launches traced: 56 us -> 55.1 us
  Pallas kernels: 55.2 us -> 54.3 us
    pallas_call x1, Pallas kernels: 54 us -> 53.1 us  [shards(): pl.pallas_call(functools.partial(kernel, n, seqs, width), out_shape=[pltp...]
where the time goes in v6:
time: 56.2 us; the launch traced here: 55.1 us
  Pallas kernels  54.3 us (97%)
  between operations  0.84 us (1%)
    pallas_call x1, Pallas kernels, shards(): pl.pallas_call(functools.partial(kernel, n, seqs, width), out_shape=[pltp...  53.1 us
    pallas_call x1, Pallas kernels, shards(): pl.pallas_call(move, out_shape=[jax.ShapeDtypeStruct(part.shape, bf16) fo...  1.16 us

profile of v6, /device:TPU:23, one launch (start us, length us, event | category | flops | bytes accessed | tf_op | source)
XLA Modules:
  0.0 55.1 jit_solution(18088737870477604712)
XLA Ops:
  0.6 53.1 %shard_map.94 = (bf16[128,4096]{1,0:T(8,128)(2,1)S(1)}, bf16[128,1024]{1,0:T(8,128)(2,1)S(1)}, bf16[128,1024]{1,0:T(8,128)(2,1)S(1)}) custom-call(bf16[128,4096]{1,0:T(8,128)(2,1)} %q_in.1, bf16[128,4096]{1,0:T(8,128)(2,1)} %e_in.1, bf16[128,4096]{1,0:T(8,128)(2,1)} %o_in.1, bf16[128,1024]{1,0:T(8,128)(2,1)} %k_in.1, bf16[128,1024]{1,0:T(8,128)(2,1)} %v_in.1, ...), custom_call_target="tpu_custom_call" | custom-call | tf_op jit(solution)/shard_map/pallas_call | solution.py:508
  53.8 1.2 %shard_map.95 = (bf16[128,4096]{1,0:T(8,128)(2,1)}, bf16[128,1024]{1,0:T(8,128)(2,1)}, bf16[128,1024]{1,0:T(8,128)(2,1)}) custom-call(bf16[128,4096]{1,0:T(8,128)(2,1)S(1)} %get-tuple-element.6.refs_0_, bf16[128,1024]{1,0:T(8,128)(2,1)S(1)} %get-tuple-element.7.refs_1_, bf16[128,1024]{1,0:T(8,128)(2,1)S(1)} %get-tuple-element.8.refs_2_), custom_call_target="tpu_custom_call" | custom-call | tf_op jit(solution)/shard_map/pallas_call | solution.py:549
